TPU v7x, 32 devices: a whole 2x2x4 slice. The times are simulated.
32 devices in a mesh: seq: 8 (over y, x, core), head: 4 (over z).
Axes of the slice: x: 2, y: 2, z: 4, core: 2. Of those that a mesh axis runs over, the one named last changes fastest.
Arguments:
- latent: bfloat16 [1024, 1024], P('seq'), may hold values from -15 to 15
- probe: bfloat16 [1024, 1024], P('seq'), may hold values from -6 to 6
- time_embed: float32 [1024], replicated, may hold values from -6 to 6
- gain_attn: float32 [1024], replicated, may hold values from 0.1 to 1.9
- w_query: bfloat16 [1024, 1024], P(None, 'head'), may hold values from -0.625 to 0.625
- w_key: bfloat16 [1024, 1024], P(None, 'head'), may hold values from -11 to 11
- w_value: bfloat16 [1024, 1024], P(None, 'head'), may hold values from -0.1875 to 0.1875
- w_out: bfloat16 [1024, 1024], P('head'), may hold values from -0.1875 to 0.1875
- gain_mlp: float32 [1024], replicated, may hold values from 0.1 to 1.9
- w_in: bfloat16 [1024, 4096], P(None, 'head'), may hold values from -0.1875 to 0.1875
- w_down: bfloat16 [4096, 1024], P('head'), may hold values from -0.09375 to 0.09375
Outputs:
- latent_end: float32 [1024, 1024], P('seq')
- frame_trace: float32 [1024], P('seq')
- frame_logp: float32 [1024], P('seq')
- mean_logp: float32 [], replicated
All inputs are finite; a program needn't handle non-finite values.
Results may differ from a plain program's by a relative error of at most 0.03.
The roundings to bfloat16 on the way count: a program that leaves them out, or rounds other values in their place, can miss the bound.
Values may be sent and summed in bfloat16 or wider, within the bound.
A program may use at most 64 MiB of HBM per device.

v0:
```python
import math

import jax
import jax.numpy as jnp
from jax import lax
from jax.sharding import PartitionSpec as P

HEAD_DIM = 64
STEPS = 2


EPSILON = 1e-05
GELU_COEF = 0.044715
ROOT_TWO_PI = math.sqrt(2.0 / math.pi)


def norm_pair(values, tangent, norm_gain):
    meansq = jnp.mean(values * values, axis=-1, keepdims=True) + EPSILON
    inverse = lax.rsqrt(meansq)
    inner_mean = jnp.mean(values * tangent, axis=-1, keepdims=True)
    primal = values * inverse * norm_gain
    derived = (tangent * inverse - values * inverse**3 * inner_mean) * norm_gain
    return (primal.astype(jnp.bfloat16), derived.astype(jnp.bfloat16))


def gelu_pair(pre_act, tangent):
    cubic_arg = pre_act + GELU_COEF * pre_act**3
    tanh_value = jnp.tanh(ROOT_TWO_PI * cubic_arg)
    output = 0.5 * pre_act * (1.0 + tanh_value)
    slope_value = 0.5 * (1.0 + tanh_value) + 0.5 * pre_act * (
        1.0 - tanh_value * tanh_value
    ) * ROOT_TWO_PI * (1.0 + 3.0 * GELU_COEF * pre_act * pre_act)
    return (output.astype(jnp.bfloat16), (slope_value * tangent).astype(jnp.bfloat16))


def split_heads(matrix):
    return matrix.reshape(matrix.shape[0], -1, HEAD_DIM)


def score_pair(queries, query_tang, keys, key_tang):
    scale = HEAD_DIM ** (-0.5)
    scores = jnp.einsum("rhd,shd->hrs", queries, keys, preferred_element_type=jnp.float32) * scale
    score_tang = (
        jnp.einsum("rhd,shd->hrs", query_tang, keys, preferred_element_type=jnp.float32)
        + jnp.einsum("rhd,shd->hrs", queries, key_tang, preferred_element_type=jnp.float32)
    ) * scale
    return (scores, score_tang)


def attention(queries, query_tang, keys, vals, key_tang, val_tang):
    rows = queries.shape[0]
    local_cols = queries.shape[1]
    head_count = local_cols // HEAD_DIM
    query_heads = split_heads(queries)
    query_tang_heads = split_heads(query_tang)
    top_start = jnp.full((head_count, rows), -1e30, jnp.float32)
    piece = (
        lax.all_gather(keys, "seq", axis=0, tiled=True),
        lax.all_gather(vals, "seq", axis=0, tiled=True),
    )
    keys_piece = split_heads(piece[0])
    vals_piece = split_heads(piece[1])
    scale = HEAD_DIM ** (-0.5)
    scores = (
        jnp.einsum("rhd,shd->hrs", query_heads, keys_piece, preferred_element_type=jnp.float32)
        * scale
    )
    new_top = jnp.maximum(top_start, jnp.max(scores, axis=-1))
    weights = jnp.exp(scores - new_top[:, :, None])
    total = jnp.sum(weights, axis=-1)
    add_primal = jnp.einsum(
        "hrs,shd->rhd", weights.astype(jnp.bfloat16), vals_piece, preferred_element_type=jnp.float32
    )
    row_top, total, acc_primal = (new_top, total, add_primal)
    piece = (
        lax.all_gather(keys, "seq", axis=0, tiled=True),
        lax.all_gather(vals, "seq", axis=0, tiled=True),
        lax.all_gather(key_tang, "seq", axis=0, tiled=True),
        lax.all_gather(val_tang, "seq", axis=0, tiled=True),
    )
    keys_piece = split_heads(piece[0])
    vals_piece = split_heads(piece[1])
    key_tang_piece = split_heads(piece[2])
    val_tang_piece = split_heads(piece[3])
    scores, score_tang = score_pair(query_heads, query_tang_heads, keys_piece, key_tang_piece)
    weights = jnp.exp(scores - row_top[:, :, None])
    weighted = weights * score_tang
    rounded = weights.astype(jnp.bfloat16)
    rounded_tang = weighted.astype(jnp.bfloat16)
    add_tang = jnp.einsum(
        "hrs,shd->rhd", rounded_tang, vals_piece, preferred_element_type=jnp.float32
    ) + jnp.einsum("hrs,shd->rhd", rounded, val_tang_piece, preferred_element_type=jnp.float32)
    carried = jnp.sum(weighted, axis=-1)
    total_t = jnp.transpose(total)[:, :, None]
    carried_t = jnp.transpose(carried)[:, :, None]
    primal = acc_primal / total_t
    tangent = add_tang / total_t - carried_t / total_t * primal
    return (
        primal.reshape(rows, local_cols).astype(jnp.bfloat16),
        tangent.reshape(rows, local_cols).astype(jnp.bfloat16),
    )


def attend_rows(normed, normed_tang, w_query, w_key, w_value):
    rows = normed.shape[0]
    stacked = jnp.concatenate([normed, normed_tang], axis=0)

    def project(weight):
        both = jnp.dot(stacked, weight, preferred_element_type=jnp.float32).astype(jnp.bfloat16)
        return (both[:rows], both[rows:])

    queries, query_tang = project(w_query)
    keys, key_tang = project(w_key)
    vals, val_tang = project(w_value)
    return attention(queries, query_tang, keys, vals, key_tang, val_tang)


def hidden_pair(normed_mlp, normed_mlp_tang, w_in):
    rows = normed_mlp.shape[0]
    pre_both = jnp.dot(
        jnp.concatenate([normed_mlp, normed_mlp_tang], axis=0),
        w_in,
        preferred_element_type=jnp.float32,
    )
    return gelu_pair(pre_both[:rows], pre_both[rows:])


def whole_field(
    inputs, direction, gain_attn, w_query, w_key, w_value, w_out, gain_mlp, w_in, w_down
):
    rows = inputs.shape[0]
    normed, normed_tang = norm_pair(inputs, direction, gain_attn)
    head_out, head_tang = attend_rows(normed, normed_tang, w_query, w_key, w_value)
    attn_terms = jnp.dot(
        jnp.concatenate([head_out, head_tang], axis=0), w_out, preferred_element_type=jnp.float32
    )
    attn_both = lax.psum(attn_terms, "head")
    attn = attn_both[:rows]
    attn_tang = attn_both[rows:]
    middle = inputs + attn
    middle_tang = direction + attn_tang
    normed_mlp, normed_mlp_tang = norm_pair(middle, middle_tang, gain_mlp)
    activ, activ_tang = hidden_pair(normed_mlp, normed_mlp_tang, w_in)
    mlp_terms = jnp.dot(
        jnp.concatenate([activ, activ_tang], axis=0), w_down, preferred_element_type=jnp.float32
    )
    mlp_both = lax.psum(mlp_terms, "head")
    return (attn + mlp_both[:rows], attn_tang + mlp_both[rows:])


def per_device(
    latent, probe, time_embed, gain_attn, w_query, w_key, w_value, w_out, gain_mlp, w_in, w_down
):
    rows = latent.shape[0]
    width = latent.shape[1]
    state = latent.astype(jnp.float32)
    direction = probe.astype(jnp.float32)
    trace = jnp.zeros((rows,), jnp.float32)
    for euler_step in range(STEPS):
        inputs = state + euler_step / STEPS * time_embed
        field, field_tang = whole_field(
            inputs, direction, gain_attn, w_query, w_key, w_value, w_out, gain_mlp, w_in, w_down
        )
        trace = trace + jnp.sum(direction * field_tang, axis=-1) / (STEPS * width)
        state = state + field / STEPS
    frame_logp = (
        trace - 0.5 * jnp.sum(state * state, axis=-1) / width - 0.5 * math.log(2.0 * math.pi)
    )
    grand_total = lax.psum(jnp.sum(frame_logp), "seq")
    mean_logp = grand_total / (rows * lax.axis_size("seq"))
    return (state, trace, frame_logp, mean_logp)


def solution(mesh):
    return jax.shard_map(
        per_device,
        mesh=mesh,
        in_specs=(
            P("seq", None),
            P("seq", None),
            P(),
            P(),
            P(None, "head"),
            P(None, "head"),
            P(None, "head"),
            P("head", None),
            P(),
            P(None, "head"),
            P("head", None),
        ),
        out_specs=(P("seq", None), P("seq"), P("seq"), P()),
        check_vma=False,
    )
```

profile of v0, /device:TPU:0, one launch (start us, length us, event | category | flops | bytes accessed | tf_op | source)
XLA Modules:
  0.0 390.4 jit_solution(14046082699471560486)
XLA Ops:
  8.1 1.2 fusion.22
  9.3 1.3 fusion.24
  10.7 1.5 convolution_convert_fusion.3
  12.2 11.3 %all_gather.29 = bf16[1024,256]{1,0:T(8,128)(2,1)S(1)} all-gather(bf16[128,256]{1,0:T(8,128)(2,1)S(1)} %get-tuple-element.42), channel_id=1, replica_groups=mesh['seq'=8,'head'=4] {'seq'}, dimensions={0}, use_global_device_ids=true | all-gather | bytes 589824 | tf_op jit(solution)/shard_map/all_gather | solution.py:58
  23.8 1.5 convolution_convert_fusion.4
  25.3 1.8 multiply_reduce_fusion.1
  27.1 1.8 fusion.113
  28.9 9.8 %all_gather.30 = bf16[1024,256]{1,0:T(8,128)(2,1)S(1)} all-gather(bf16[128,256]{1,0:T(8,128)(2,1)S(1)} %get-tuple-element.41), channel_id=1, replica_groups=mesh['seq'=8,'head'=4] {'seq'}, dimensions={0}, use_global_device_ids=true | all-gather | bytes 589824 | tf_op jit(solution)/shard_map/all_gather | solution.py:78
  38.9 1.5 convolution_convert_fusion.5
  40.4 9.9 %all_gather.28 = bf16[1024,256]{1,0:T(8,128)(2,1)} all-gather(bf16[128,256]{1,0:T(8,128)(2,1)S(1)} %get-tuple-element.40), channel_id=1, replica_groups=mesh['seq'=8,'head'=4] {'seq'}, dimensions={0}, use_global_device_ids=true | all-gather | bytes 589824 | tf_op jit(solution)/shard_map/all_gather | solution.py:59
  50.4 1.2 copy.27
  51.6 2.2 fusion
  53.9 2.5 fusion.109
  58.1 10.7 %all_gather.31 = bf16[1024,256]{1,0:T(8,128)(2,1)} all-gather(bf16[128,256]{1,0:T(8,128)(2,1)S(1)} %get-tuple-element.39), channel_id=1, replica_groups=mesh['seq'=8,'head'=4] {'seq'}, dimensions={0}, use_global_device_ids=true | all-gather | bytes 589824 | tf_op jit(solution)/shard_map/all_gather | solution.py:79
  68.8 1.3 copy.30
  70.1 2.2 fusion.12
  72.4 1.4 fusion.77
  73.8 52.3 %all-reduce.5.cloned.1.call-done = f32[256,1024]{1,0:T(8,128)} async-done(((f32[256,1024]{1,0:T(8,128)}), f32[256,1024]{1,0:T(8,128)}) %all-reduce.5.cloned.1.call-update) | async-done | bytes 1048592 | tf_op jit(solution)/shard_map/psum | solution.py:137
  126.1 1.6 multiply_reduce_fusion.7
  127.7 1.2 multiply_convert_fusion.6
  130.5 1.7 fusion.61
  132.3 51.3 %all-reduce.7.cloned.1.call-done = f32[256,1024]{1,0:T(8,128)} async-done(((f32[256,1024]{1,0:T(8,128)}), f32[256,1024]{1,0:T(8,128)}) %all-reduce.7.cloned.1.call-update) | async-done | bytes 1048592 | tf_op jit(solution)/shard_map/psum | solution.py:147
  183.6 1.4 multiply_reduce_fusion.5
  185.7 1.0 convolution_convert_fusion.1
  187.7 11.0 %all_gather.33 = bf16[1024,256]{1,0:T(8,128)(2,1)} all-gather(bf16[128,256]{1,0:T(8,128)(2,1)S(1)} %get-tuple-element.36), channel_id=1, replica_groups=mesh['seq'=8,'head'=4] {'seq'}, dimensions={0}, use_global_device_ids=true | all-gather | bytes 589824 | tf_op jit(solution)/shard_map/all_gather | solution.py:58
  198.7 2.0 copy.32
  201.7 2.9 multiply_reduce_fusion
  204.6 1.8 fusion.114
  206.3 10.7 %all_gather.34 = bf16[1024,256]{1,0:T(8,128)(2,1)} all-gather(bf16[128,256]{1,0:T(8,128)(2,1)S(1)} %get-tuple-element.35), channel_id=1, replica_groups=mesh['seq'=8,'head'=4] {'seq'}, dimensions={0}, use_global_device_ids=true | all-gather | bytes 589824 | tf_op jit(solution)/shard_map/all_gather | solution.py:78
  217.0 2.1 copy.33
  219.1 1.5 fusion.103
  220.6 9.9 %all_gather.32 = bf16[1024,256]{1,0:T(8,128)(2,1)} all-gather(bf16[128,256]{1,0:T(8,128)(2,1)S(1)} %get-tuple-element.34), channel_id=1, replica_groups=mesh['seq'=8,'head'=4] {'seq'}, dimensions={0}, use_global_device_ids=true | all-gather | bytes 589824 | tf_op jit(solution)/shard_map/all_gather | solution.py:59
  230.5 2.1 copy.31
  232.6 2.2 fusion.2
  234.8 2.7 fusion.111
  238.2 1.2 fusion.112
  239.4 1.1 fusion.14
  240.5 10.7 %all_gather.35 = bf16[1024,256]{1,0:T(8,128)(2,1)} all-gather(bf16[128,256]{1,0:T(8,128)(2,1)S(1)} %copy-done.16), channel_id=1, replica_groups=mesh['seq'=8,'head'=4] {'seq'}, dimensions={0}, use_global_device_ids=true | all-gather | bytes 589824 | tf_op jit(solution)/shard_map/all_gather | solution.py:79
  251.2 2.0 copy.34
  253.2 2.4 fusion.13
  255.6 1.4 fusion.81
  257.1 50.3 %all-reduce.9.cloned.1.call-done = f32[256,1024]{1,0:T(8,128)} async-done(((f32[256,1024]{1,0:T(8,128)}), f32[256,1024]{1,0:T(8,128)}) %all-reduce.9.cloned.1.call-update) | async-done | bytes 1048592 | tf_op jit(solution)/shard_map/psum | solution.py:137
  307.4 1.9 multiply_reduce_fusion.4
  311.2 1.7 fusion.69
  312.9 51.3 %all-reduce.11.cloned.1.call-done = f32[256,1024]{1,0:T(8,128)} async-done(((f32[256,1024]{1,0:T(8,128)}), f32[256,1024]{1,0:T(8,128)}) %all-reduce.11.cloned.1.call-update) | async-done | bytes 1048592 | tf_op jit(solution)/shard_map/psum | solution.py:147
  364.2 2.5 multiply_reduce_fusion.2
  366.7 1.1 fusion.101
  367.8 14.3 %psum.39 = f32[]{:T(128)} all-reduce(f32[]{:T(128)} %get-tuple-element.13), channel_id=1, replica_groups=mesh['seq'=8,'head'=4] {'seq'}, use_global_device_ids=true, to_apply=%region_22.0 | all-reduce | flops 1 | bytes 8 | tf_op jit(solution)/shard_map/psum | solution.py:169
  (83 shorter events, 9.8 us)
Async XLA Ops:
  7.2 121.8 %copy-start = (bf16[1024,1024]{1,0:T(8,128)(2,1)S(1)}, bf16[1024,1024]{1,0:T(8,128)(2,1)}, u32[]{:S(2)}) copy-start(bf16[1024,1024]{1,0:T(8,128)(2,1)} %param.20) | copy-start | bytes 6291460
  7.2 118.9 %all-reduce.5.cloned.1.call-start = ((), (), s32[]{:S(2)}) async-start(), calls=%async_computation | async-start | bytes 2097152 | tf_op jit(solution)/shard_map/psum | solution.py:137
  10.6 1.6 copy-start.15
  10.7 13.1 %copy-start.14 = (bf16[128,1024]{1,0:T(8,128)(2,1)}, bf16[128,1024]{1,0:T(8,128)(2,1)S(1)}, u32[]{:S(2)}) copy-start(bf16[128,1024]{1,0:T(8,128)(2,1)S(1)} %get-tuple-element.31) | copy-start | bytes 786436
  51.6 2.2 copy-start.1
  68.8 3.5 copy-start.12
  72.3 53.7 %copy-start.3 = (bf16[128,1024]{1,0:T(8,128)(2,1)S(1)}, bf16[128,1024]{1,0:T(8,128)(2,1)}, u32[]{:S(2)}) copy-start(bf16[128,1024]{1,0:T(8,128)(2,1)} %param.12) | copy-start | bytes 786436
  72.4 55.3 %copy-start.19 = (f32[1024]{0:T(1024)S(1)}, f32[1024]{0:T(1024)}, u32[]{:S(2)}) copy-start(f32[1024]{0:T(1024)} %param.19) | copy-start | bytes 12292
  73.7 109.8 %all-reduce.7.cloned.1.call-start = ((), (), s32[]{:S(2)}) async-start(), calls=%async_computation.1 | async-start | bytes 2097152 | tf_op jit(solution)/shard_map/psum | solution.py:147
  126.1 1.6 copy-start.4
  128.9 1.6 copy-start.5
  132.2 52.8 %copy-start.18 = (f32[1024]{0:T(1024)S(1)}, f32[1024]{0:T(1024)}, u32[]{:S(2)}) copy-start(f32[1024]{0:T(1024)} %param.14) | copy-start | bytes 12292
  132.3 175.1 %all-reduce.9.cloned.1.call-start = ((), (), s32[]{:S(2)}) async-start(), calls=%async_computation.2 | async-start | bytes 2097152 | tf_op jit(solution)/shard_map/psum | solution.py:137
  183.6 1.8 copy-start.20
  183.6 2.1 copy-start.21
  185.0 1.7 copy-start.7
  185.1 1.6 copy-start.22
  200.7 3.8 copy-start.11
  232.6 2.2 copy-start.2
  234.8 3.4 copy-start.10
  238.2 2.3 copy-start.16
  253.2 2.4 copy-start.13
  253.2 2.4 copy-start.17
  257.0 107.2 %all-reduce.11.cloned.1.call-start = ((), (), s32[]{:S(2)}) async-start(), calls=%async_computation.3 | async-start | bytes 2097152 | tf_op jit(solution)/shard_map/psum | solution.py:147
  307.4 1.9 copy-start.9
  309.6 1.6 copy-start.6
  311.2 53.0 %copy-start.8 = (f32[128,1024]{1,0:T(8,128)S(1)}, f32[128,1024]{1,0:T(8,128)}, u32[]{:S(2)}) copy-start(f32[128,1024]{1,0:T(8,128)} %copy-done.7) | copy-start | bytes 1572868
Sparse Core Ops, SparseCore 0:
  73.9 52.1 all-reduce.4
  132.4 51.1 all-reduce.6
  257.1 50.2 all-reduce.8
  313.0 51.1 all-reduce.10
where the time goes:
time: 391 us; the launch traced here: 390 us
  waiting for transfers between devices  205 us (52%)
  blocking collectives  98.5 us (25%)
  matrix products  35.8 us (9%)
  other arithmetic  20.1 us (5%)
  between operations  16 us (4%)
  local copies, waits for them, and re-layouts  14.7 us (4%)
    psum x2, waiting for transfers between devices, whole_field(): attn_both = lax.psum(attn_terms, 'head')  103 us
    psum x2, waiting for transfers between devices, whole_field(): mlp_both = lax.psum(mlp_terms, 'head')  103 us
    all_gather x2, blocking collectives, attention(): lax.all_gather(keys, 'seq', axis=0, tiled=True)  22.4 us
    all_gather x2, blocking collectives, attention(): lax.all_gather(val_tang, 'seq', axis=0, tiled=True)  21.4 us
    all_gather x2, blocking collectives, attention(): lax.all_gather(key_tang, 'seq', axis=0, tiled=True)  20.5 us
    all_gather x2, blocking collectives, attention(): lax.all_gather(vals, 'seq', axis=0, tiled=True)  19.9 us
    psum x1, blocking collectives, per_device(): grand_total = lax.psum(jnp.sum(frame_logp), 'seq')  14.3 us
  transfers between devices with their start and end apart: 4, of which 4 were waited for; matrix products, arithmetic and copies ran while one was open for 0% of the time, Pallas kernels for 0%

commit v1 on v0

v1 whole, which is shorter than its diff:
```python
import functools
import math

import jax
import jax.numpy as jnp
from jax import lax
from jax.experimental import pallas as pl
from jax.experimental.pallas import tpu as pltpu
from jax.sharding import PartitionSpec as P

HEAD_DIM = 64
STEPS = 2
EPSILON = 1e-05
GELU_COEF = 0.044715
ROOT_TWO_PI = math.sqrt(2.0 / math.pi)
LANES = 128
BF16 = jnp.bfloat16
F32 = jnp.float32


def norm_pair(values, tangent, norm_gain):
    meansq = jnp.mean(values * values, axis=-1, keepdims=True) + EPSILON
    inverse = lax.rsqrt(meansq)
    inner_mean = jnp.mean(values * tangent, axis=-1, keepdims=True)
    primal = values * inverse * norm_gain
    derived = (tangent * inverse - values * (inverse * inverse * inverse * inner_mean)) * norm_gain
    return (primal.astype(BF16), derived.astype(BF16))


def gelu_pair(pre_act, tangent):
    square = pre_act * pre_act
    tanh_value = jnp.tanh(ROOT_TWO_PI * pre_act * (1.0 + GELU_COEF * square))
    half = 0.5 * (1.0 + tanh_value)
    slope_value = half + 0.5 * pre_act * (1.0 - tanh_value * tanh_value) * (
        ROOT_TWO_PI * (1.0 + 3.0 * GELU_COEF * square)
    )
    return ((pre_act * half).astype(BF16), (slope_value * tangent).astype(BF16))


def dot(a, b):
    return jnp.dot(a, b, preferred_element_type=F32)


def dot_t(a, b):
    return lax.dot_general(a, b, (((1,), (1,)), ((), ())), preferred_element_type=F32)


def flow_kernel(
    n,
    m,
    latent,
    probe,
    time_embed,
    gain_attn,
    gain_mlp,
    w_query,
    w_key,
    w_value,
    w_out,
    w_in,
    w_down,
    latent_end,
    stats_out,
    mean_out,
    wqkv,
    wout,
    win,
    wdown,
    normed,
    qbuf,
    kbuf,
    vbuf,
    headbuf,
    headsend,
    headall,
    midbuf,
    partial,
    rssend,
    rsrecv,
    state,
    statbuf,
    sumbuf,
    wsem,
    wsend,
    wrecv,
    kvsend,
    kvrecv,
    zsend,
    zrecv,
    ssend,
    srecv,
    msend,
    mrecv,
):
    s = lax.axis_index("seq")
    z = lax.axis_index("head")
    rows, width = latent.shape
    part = rows // m
    cols = w_query.shape[1]
    pairs = cols // LANES

    def flip(bit):
        return s + bit - 2 * bit * lax.rem(s // bit, 2)

    def zpeer(d):
        return lax.rem(z + d, m)

    def zfrom(d):
        return lax.rem(z + m - d, m)

    def remote(src, dst, send, recv, target_s, target_z):
        return pltpu.make_async_remote_copy(
            src_ref=src,
            dst_ref=dst,
            send_sem=send,
            recv_sem=recv,
            device_id=(target_s, target_z),
            device_id_type=pl.DeviceIdType.MESH,
        )

    loads = [
        pltpu.make_async_copy(w_query, wqkv.at[:, pl.ds(0, cols)], wsem.at[0]),
        pltpu.make_async_copy(w_key, wqkv.at[:, pl.ds(cols, cols)], wsem.at[1]),
        pltpu.make_async_copy(w_value, wqkv.at[:, pl.ds(2 * cols, cols)], wsem.at[2]),
        pltpu.make_async_copy(w_out, wout.at[z], wsem.at[3]),
        pltpu.make_async_copy(w_in, win, wsem.at[4]),
        pltpu.make_async_copy(w_down, wdown, wsem.at[5]),
    ]
    for load in loads:
        load.start()

    barrier = pltpu.get_barrier_semaphore()
    for d in range(1, m):
        pl.semaphore_signal(
            barrier, inc=1, device_id=(s, zpeer(d)), device_id_type=pl.DeviceIdType.MESH
        )
    for d in range(1, n):
        pl.semaphore_signal(
            barrier,
            inc=1,
            device_id=(lax.rem(s + d, n), z),
            device_id_type=pl.DeviceIdType.MESH,
        )

    def put_pair(ref, j, pair):
        ref[j, :part, :] = pair[0]
        ref[j, part:, :] = pair[1]

    for j in range(m):
        span = slice(j * part, (j + 1) * part)
        put_pair(
            normed.at[0],
            j,
            norm_pair(latent[span, :].astype(F32), probe[span, :].astype(F32), gain_attn[...]),
        )
    own = pl.ds(pl.multiple_of(z * part, part), part)
    direction = probe[own, :].astype(F32)
    state[...] = latent[own, :].astype(F32)

    pl.semaphore_wait(barrier, n + m - 2)

    half = cols // 2
    core = lax.rem(s, 2)
    mine = pl.ds(pl.multiple_of(core * half, half), half)
    other = pl.ds(pl.multiple_of((1 - core) * half, half), half)
    partner = flip(1)
    loads[3].wait()
    w_copies = []
    for d in range(1, m):
        copy = remote(
            wout.at[z, mine], wout.at[z, mine], wsend.at[0, d], wrecv.at[0, d], s, zpeer(d)
        )
        copy.start()
        w_copies.append(copy)

    def kv_exchange(k):
        bufs = (kbuf, vbuf)
        sends = []

        def give(which, rel, slot, target, at):
            copy = remote(
                bufs[which].at[k, slot],
                bufs[which].at[k, slot],
                kvsend.at[k, which, len(sends)],
                kvrecv.at[k, which, at],
                target,
                z,
            )
            copy.start()
            sends.append(copy)

        def got(which, slot, at):
            pltpu.make_async_copy(
                bufs[which].at[k, slot], bufs[which].at[k, slot], kvrecv.at[k, which, at]
            ).wait()

        if n == 8:
            xn, yn, dn = flip(2), flip(4), lax.rem(s + 4, 8)
            dn = dn + 2 - 4 * lax.rem(dn // 2, 2)
            give(0, 0, s, xn, 2)
            give(1, 0, s, yn, 4)
            give(0, 0, s, yn, 4)
            give(1, 0, s, xn, 2)
            give(0, 0, s, partner, 1)
            give(1, 0, s, partner, 1)
            got(0, xn, 2)
            give(0, 2, xn, yn, 6)
            give(0, 2, xn, partner, 3)
            got(1, yn, 4)
            give(1, 4, yn, xn, 6)
            give(1, 4, yn, partner, 5)
            got(0, yn, 4)
            give(0, 4, yn, partner, 5)
            got(1, xn, 2)
            give(1, 2, xn, partner, 3)
            got(0, dn, 6)
            give(0, 6, dn, partner, 7)
            got(1, dn, 6)
            give(1, 6, dn, partner, 7)

            def across(base):
                return base + 1 - 2 * lax.rem(base, 2)

            keys_left = [(0, across(t), r) for t, r in ((s, 1), (xn, 3), (yn, 5), (dn, 7))]
            vals_left = [(1, across(t), r) for t, r in ((s, 1), (xn, 3), (yn, 5), (dn, 7))]
        else:
            for d in range(1, n):
                for which in range(2):
                    give(which, d, s, lax.rem(s + d, n), d)
            keys_left = [(0, lax.rem(s + n - d, n), d) for d in range(1, n)]
            vals_left = [(1, lax.rem(s + n - d, n), d) for d in range(1, n)]
        return sends, keys_left, vals_left, got

    lane = lax.broadcasted_iota(jnp.int32, (1, LANES), 1)
    scale = HEAD_DIM ** (-0.5)
    frames = rows * n

    for k in range(STEPS):
        if k == 0:
            for load in loads[:3]:
                load.wait()
        stacked = normed[k].reshape(2 * rows, width)

        def project(which):
            both = dot(stacked, wqkv[:, which * cols : (which + 1) * cols]).astype(BF16)
            both = both.reshape(m, 2, part, cols)
            return both[:, 0].reshape(rows, cols), both[:, 1].reshape(rows, cols)

        for which, ref in ((1, kbuf), (2, vbuf)):
            prim, tang = project(which)
            ref[k, s, 0] = prim
            ref[k, s, 1] = tang
        sends, keys_left, vals_left, got = kv_exchange(k)
        prim, tang = project(0)
        qbuf[0] = prim
        qbuf[1] = tang
        for item in keys_left + vals_left:
            got(*item)

        @pl.loop(0, pairs)
        def _(p):
            at = pl.ds(pl.multiple_of(p * LANES, LANES), LANES)
            keys = kbuf[k, :, 0, :, at].reshape(frames, LANES)
            key_tang = kbuf[k, :, 1, :, at].reshape(frames, LANES)
            vals = vbuf[k, :, 0, :, at].reshape(frames, LANES)
            val_tang = vbuf[k, :, 1, :, at].reshape(frames, LANES)
            both_keys = jnp.concatenate([keys, key_tang], axis=1)
            both_vals = jnp.concatenate([vals, val_tang], axis=1)
            queries = qbuf[0, :, at]
            query_tang = qbuf[1, :, at]
            zero = jnp.zeros_like(queries)
            prims, tangs = [], []
            for side in range(LANES // HEAD_DIM):
                keep = (lane // HEAD_DIM) == side
                q = jnp.where(keep, queries, zero)
                qt = jnp.where(keep, query_tang, zero)
                left = jnp.concatenate(
                    [jnp.concatenate([q, zero], axis=1), jnp.concatenate([qt, q], axis=1)], axis=0
                )
                both = dot_t(left, both_keys) * scale
                scores, score_tang = both[:rows], both[rows:]
                weights = jnp.exp(scores - jnp.max(scores, axis=-1, keepdims=True))
                weighted = weights * score_tang
                total = jnp.sum(weights, axis=-1, keepdims=True)
                carried = jnp.sum(weighted, axis=-1, keepdims=True)
                rounded = jnp.concatenate([weights.astype(BF16), weighted.astype(BF16)], axis=0)
                mixed = dot(rounded, both_vals)
                prim = mixed[:rows, :LANES] / total
                tang = (mixed[rows:, :LANES] + mixed[:rows, LANES:]) / total - (
                    carried / total
                ) * prim
                prims.append(prim)
                tangs.append(tang)
            first = (lane // HEAD_DIM) == 0
            headbuf[0, :, at] = jnp.where(first, prims[0], prims[1]).astype(BF16)
            headbuf[1, :, at] = jnp.where(first, tangs[0], tangs[1]).astype(BF16)

        for j in range(m):
            headsend[k, j, :part, :] = headbuf[0, j * part : (j + 1) * part, :]
            headsend[k, j, part:, :] = headbuf[1, j * part : (j + 1) * part, :]

        def z_start(phase, src_of, dst):
            copies = []
            for d in range(m - 1, 0, -1):
                copy = remote(
                    src_of(zpeer(d)),
                    dst,
                    zsend.at[k, phase, d],
                    zrecv.at[k, phase, d],
                    s,
                    zpeer(d),
                )
                copy.start()
                copies.append(copy)
            return copies

        def z_wait(copies):
            for copy in copies:
                copy.wait_send()
                copy.wait_recv()

        copies = z_start(0, lambda j: headsend.at[k, j], headall.at[k, z])
        headall[k, z] = headsend[k, z]
        if k == 0:
            forwards = []
            for d, copy in zip(range(1, m), w_copies):
                copy.wait_send()
                copy.wait_recv()
                forward = remote(
                    wout.at[zfrom(d), mine],
                    wout.at[zfrom(d), mine],
                    wsend.at[1, d],
                    wrecv.at[1, d],
                    partner,
                    z,
                )
                forward.start()
                forwards.append(forward)
            for forward in forwards:
                forward.wait_send()
                forward.wait_recv()
        z_wait(copies)
        attn_both = jnp.zeros((2 * part, width), F32)
        for j in range(m):
            attn_both = attn_both + dot(headall[k, j], wout[j])
        inputs = state[...]
        if k > 0:
            inputs = inputs + (k / STEPS) * time_embed[...]
        put_pair(
            midbuf.at[k],
            z,
            norm_pair(inputs + attn_both[:part], direction + attn_both[part:], gain_mlp[...]),
        )
        copies = z_start(1, lambda j: midbuf.at[k, z], midbuf.at[k, z])
        if k == 0:
            loads[4].wait()
            loads[5].wait()
        z_wait(copies)
        pre = dot(midbuf[k].reshape(2 * rows, width), win[...]).reshape(m, 2, part, win.shape[1])
        act, act_tang = gelu_pair(pre[:, 0], pre[:, 1])
        acts = jnp.concatenate([act, act_tang], axis=1).reshape(2 * rows, win.shape[1])
        partial[...] = dot(acts, wdown[...]).reshape(m, 2 * part, width)
        rssend[k] = partial[...].astype(BF16)
        copies = z_start(2, lambda j: rssend.at[k, j], rsrecv.at[k, z])
        z_wait(copies)
        both = attn_both + partial[z]
        for d in range(1, m):
            both = both + rsrecv[k, zfrom(d)].astype(F32)
        trace_add = jnp.sum(direction * both[part:], axis=-1, keepdims=True) / (STEPS * width)
        trace = trace_add if k == 0 else trace + trace_add
        new_state = state[...] + both[:part] / STEPS
        state[...] = new_state
        last = k == STEPS - 1
        if not last:
            following = new_state + ((k + 1) / STEPS) * time_embed[...]
            put_pair(normed.at[k + 1], z, norm_pair(following, direction, gain_attn[...]))
        else:
            logp = (
                trace
                - 0.5 * jnp.sum(new_state * new_state, axis=-1, keepdims=True) / width
                - 0.5 * math.log(2.0 * math.pi)
            )
            statbuf[z] = jnp.where(lane == 0, trace, logp)
            stat_copies = []
            for d in range(1, m):
                copy = remote(
                    statbuf.at[z], statbuf.at[z], ssend.at[d], srecv.at[d], s, zpeer(d)
                )
                copy.start()
                stat_copies.append(copy)
            high = new_state.astype(BF16)
            put_pair(normed.at[k + 1], z, (high, (new_state - high.astype(F32)).astype(BF16)))
        copies = z_start(3, lambda j: normed.at[k + 1, z], normed.at[k + 1, z])
        for send in sends:
            send.wait_send()
        if last:
            z_wait(stat_copies)
            stats = statbuf[...].reshape(rows, LANES)
            sumbuf[s] = jnp.broadcast_to(
                jnp.sum(stats.reshape(rows // 8, 8, LANES), axis=0), (8, LANES)
            )
            mean_copies = []
            for d in range(1, n):
                copy = remote(
                    sumbuf.at[s], sumbuf.at[s], msend.at[d], mrecv.at[d], lax.rem(s + d, n), z
                )
                copy.start()
                mean_copies.append(copy)
            stats_out[...] = jnp.transpose(stats)[:8, :]
        z_wait(copies)
    final = normed[STEPS].reshape(m, 2, part, width).astype(F32)
    latent_end[...] = (final[:, 0] + final[:, 1]).reshape(rows, width)
    z_wait(mean_copies)
    sums = jnp.sum(sumbuf[...], axis=0)
    mean_out[...] = jnp.broadcast_to(jnp.sum(sums, axis=0, keepdims=True) / frames, (8, LANES))


def per_device(
    n,
    m,
    latent,
    probe,
    time_embed,
    gain_attn,
    w_query,
    w_key,
    w_value,
    w_out,
    gain_mlp,
    w_in,
    w_down,
):
    rows, width = latent.shape
    cols = w_query.shape[1]
    hidden = w_in.shape[1]
    part = rows // m
    vmem = pl.BlockSpec(memory_space=pltpu.VMEM)
    anyspace = pl.BlockSpec(memory_space=pl.ANY)
    dma = pltpu.SemaphoreType.DMA
    state, stats, mean = pl.pallas_call(
        functools.partial(flow_kernel, n, m),
        out_shape=(
            jax.ShapeDtypeStruct((rows, width), F32),
            jax.ShapeDtypeStruct((8, rows), F32),
            jax.ShapeDtypeStruct((8, LANES), F32),
        ),
        in_specs=[vmem] * 5 + [anyspace] * 6,
        out_specs=(vmem, vmem, vmem),
        scratch_shapes=[
            pltpu.VMEM((width, 3 * cols), BF16),
            pltpu.VMEM((m, cols, width), BF16),
            pltpu.VMEM((width, hidden), BF16),
            pltpu.VMEM((hidden, width), BF16),
            pltpu.VMEM((STEPS + 1, m, 2 * part, width), BF16),
            pltpu.VMEM((2, rows, cols), BF16),
            pltpu.VMEM((STEPS, n, 2, rows, cols), BF16),
            pltpu.VMEM((STEPS, n, 2, rows, cols), BF16),
            pltpu.VMEM((2, rows, cols), BF16),
            pltpu.VMEM((STEPS, m, 2 * part, cols), BF16),
            pltpu.VMEM((STEPS, m, 2 * part, cols), BF16),
            pltpu.VMEM((STEPS, m, 2 * part, width), BF16),
            pltpu.VMEM((m, 2 * part, width), F32),
            pltpu.VMEM((STEPS, m, 2 * part, width), BF16),
            pltpu.VMEM((STEPS, m, 2 * part, width), BF16),
            pltpu.VMEM((part, width), F32),
            pltpu.VMEM((m, part, LANES), F32),
            pltpu.VMEM((n, 8, LANES), F32),
            dma((6,)),
            dma((2, m)),
            dma((2, m)),
            dma((STEPS, 2, 2 * n)),
            dma((STEPS, 2, n)),
            dma((STEPS, 4, m)),
            dma((STEPS, 4, m)),
            dma((m,)),
            dma((m,)),
            dma((n,)),
            dma((n,)),
        ],
        compiler_params=pltpu.CompilerParams(
            collective_id=0, has_side_effects=True, vmem_limit_bytes=60 * 1024 * 1024
        ),
    )(
        latent,
        probe,
        time_embed.reshape(1, width),
        gain_attn.reshape(1, width),
        gain_mlp.reshape(1, width),
        w_query,
        w_key,
        w_value,
        w_out,
        w_in,
        w_down,
    )
    return (state, stats[0], stats[1], mean[0, 1])


def solution(mesh):
    return jax.shard_map(
        functools.partial(per_device, mesh.shape["seq"], mesh.shape["head"]),
        mesh=mesh,
        in_specs=(
            P("seq", None),
            P("seq", None),
            P(),
            P(),
            P(None, "head"),
            P(None, "head"),
            P(None, "head"),
            P("head", None),
            P(),
            P(None, "head"),
            P("head", None),
        ),
        out_specs=(P("seq", None), P("seq"), P("seq"), P()),
        check_vma=False,
    )
```

time: 391 us -> 140 us (0.36)
  waiting for transfers between devices: 205 us -> 0 us
  Pallas kernels: 0 us -> 134 us
  blocking collectives: 98.5 us -> 0 us
  matrix products: 35.8 us -> 0 us
  other arithmetic: 20.1 us -> 0 us
  between operations: 16 us -> 0.64 us
  local copies, waits for them, and re-layouts: 14.7 us -> 4.41 us
    psum x4 -> x0, waiting for transfers between devices: 205 us -> none  [the longest x2 103 us: whole_field(): attn_both = lax.psum(attn_terms, 'head')]
    pallas_call x0 -> x1, Pallas kernels: none -> 134 us  [per_device(): pl.pallas_call(functools.partial(flow_kernel, n, m), out_shape=(jax.Shape...]
    all_gather x8 -> x0, blocking collectives: 84.2 us -> none  [the longest x2 22.4 us: attention(): lax.all_gather(keys, 'seq', axis=0, tiled=True)]
    dot_general x24 -> x0, matrix products: 35.8 us -> none  [the longest x6 6.74 us: project(): jnp.dot(stacked, weight, preferred_element_type=jnp.float32)]
    psum x1 -> x0, blocking collectives: 14.3 us -> none  [per_device(): grand_total = lax.psum(jnp.sum(frame_logp), 'seq')]
    reduce_sum x8 -> x0, other arithmetic: 14.2 us -> none  [the longest x4 6.19 us: norm_pair(): meansq = jnp.mean(values * values, axis=-1, keepdims=True) + EPSILON]
    all_gather x8 -> x0, local copies, waits for them, and re-layouts: 11.2 us -> none  [the longest x2 3.35 us: attention(): lax.all_gather(val_tang, 'seq', axis=0, tiled=True)]
  transfers between devices with their start and end apart: 4 -> 0, of which waited for: 4 -> 0; matrix products, arithmetic and copies ran while one was open for 0% -> 0% of each run, Pallas kernels for 0% -> 0%
where the time goes in v1:
time: 140 us
  Pallas kernels  134 us (96%)
  local copies, waits for them, and re-layouts  4.41 us (3%)
    pallas_call x1, Pallas kernels, per_device(): pl.pallas_call(functools.partial(flow_kernel, n, m), out_shape=(jax.Shape...  134 us

profile of v1, /device:TPU:0, one launch (start us, length us, event | category | flops | bytes accessed | tf_op | source)
XLA Modules:
  0.0 139.5 jit_solution(17526499170693290793)
XLA Ops:
  0.6 134.5 %shard_map.138 = (f32[128,1024]{1,0:T(8,128)}, f32[8,128]{1,0:T(8,128)}, f32[8,128]{1,0:T(8,128)}) custom-call(bf16[128,1024]{1,0:T(8,128)(2,1)} %latent.1, bf16[128,1024]{1,0:T(8,128)(2,1)} %probe.1, f32[1,1024]{1,0:T(1,128)} %bitcast.8, f32[1,1024]{1,0:T(1,128)} %bitcast.9, f32[1,1024]{1,0:T(1,128)} %bitcast.10, bf16[1024,256]{1,0:T(8,128)(2,1)} %w_query.1, ...), custom_call_target="tpu_custom_call" | custom-call | tf_op jit(solution)/shard_map/pallas_call | solution.py:440
  135.1 1.3 slice.11
  136.4 1.3 slice_bitcast_fusion
  137.6 1.9 %copy.16 = f32[128,1024]{1,0:T(8,128)} copy(f32[128,1024]{1,0:T(8,128)} %get-tuple-element.16) | data formatting | bytes 1048576

commit v2 on v1

v2 whole, which is shorter than its diff:
```python
import functools
import math

import jax
import jax.numpy as jnp
from jax import lax
from jax.experimental import pallas as pl
from jax.experimental.pallas import tpu as pltpu
from jax.sharding import PartitionSpec as P

HEAD_DIM = 64
STEPS = 2
EPSILON = 1e-05
GELU_COEF = 0.044715
ROOT_TWO_PI = math.sqrt(2.0 / math.pi)
LANES = 128
HALVES = 2
BF16 = jnp.bfloat16
F32 = jnp.float32


def norm_pair(values, tangent, norm_gain):
    meansq = jnp.mean(values * values, axis=-1, keepdims=True) + EPSILON
    inverse = lax.rsqrt(meansq)
    inner_mean = jnp.mean(values * tangent, axis=-1, keepdims=True)
    primal = values * inverse * norm_gain
    derived = (tangent * inverse - values * (inverse * inverse * inverse * inner_mean)) * norm_gain
    return (primal.astype(BF16), derived.astype(BF16))


def gelu_pair(pre_act, tangent):
    square = pre_act * pre_act
    tanh_value = jnp.tanh(ROOT_TWO_PI * pre_act * (1.0 + GELU_COEF * square))
    half = 0.5 * (1.0 + tanh_value)
    slope_value = half + 0.5 * pre_act * (1.0 - tanh_value * tanh_value) * (
        ROOT_TWO_PI * (1.0 + 3.0 * GELU_COEF * square)
    )
    return ((pre_act * half).astype(BF16), (slope_value * tangent).astype(BF16))


def dot(a, b):
    return jnp.dot(a, b, preferred_element_type=F32)


def dot_t(a, b):
    return lax.dot_general(a, b, (((1,), (1,)), ((), ())), preferred_element_type=F32)


def flow_kernel(
    n,
    m,
    latent,
    probe,
    time_embed,
    gain_attn,
    gain_mlp,
    w_query,
    w_key,
    w_value,
    w_out,
    w_in,
    w_down,
    latent_end,
    stats_out,
    mean_out,
    wqkv,
    wout,
    win,
    wdown,
    normed,
    qbuf,
    kbuf,
    vbuf,
    headall,
    inbuf,
    probe_down,
    partial,
    rssend,
    rsrecv,
    state,
    delta,
    tracebuf,
    tilebuf,
    sumbuf,
    wsem,
    wsend,
    wrecv,
    kvsend,
    kvrecv,
    zsend,
    zrecv,
    ssend,
    srecv,
    msend,
    mrecv,
):
    s = lax.axis_index("seq")
    z = lax.axis_index("head")
    rows, width = latent.shape
    hrows = rows // HALVES
    part = hrows // m
    cols = w_query.shape[1]
    pairs = cols // LANES

    def flip(bit):
        return s + bit - 2 * bit * lax.rem(s // bit, 2)

    def zpeer(d):
        return lax.rem(z + d, m)

    def zfrom(d):
        return lax.rem(z + m - d, m)

    def remote(src, dst, send, recv, target_s, target_z):
        return pltpu.make_async_remote_copy(
            src_ref=src,
            dst_ref=dst,
            send_sem=send,
            recv_sem=recv,
            device_id=(target_s, target_z),
            device_id_type=pl.DeviceIdType.MESH,
        )

    loads = [
        pltpu.make_async_copy(w_query, wqkv.at[:, pl.ds(0, cols)], wsem.at[0]),
        pltpu.make_async_copy(w_key, wqkv.at[:, pl.ds(cols, cols)], wsem.at[1]),
        pltpu.make_async_copy(w_value, wqkv.at[:, pl.ds(2 * cols, cols)], wsem.at[2]),
        pltpu.make_async_copy(w_out, wout.at[z], wsem.at[3]),
        pltpu.make_async_copy(w_in, win, wsem.at[4]),
        pltpu.make_async_copy(w_down, wdown, wsem.at[5]),
    ]
    for load in loads:
        load.start()

    barrier = pltpu.get_barrier_semaphore()
    for d in range(1, m):
        pl.semaphore_signal(
            barrier, inc=1, device_id=(s, zpeer(d)), device_id_type=pl.DeviceIdType.MESH
        )
    for d in range(1, n):
        pl.semaphore_signal(
            barrier,
            inc=1,
            device_id=(lax.rem(s + d, n), z),
            device_id_type=pl.DeviceIdType.MESH,
        )

    def own_rows(h):
        return pl.ds(pl.multiple_of(h * hrows + z * part, part), part)

    def norm_all():
        for h in range(HALVES):
            span = slice(h * hrows, (h + 1) * hrows)
            prim, tang = norm_pair(inbuf[span, :], probe[span, :].astype(F32), gain_attn[...])
            normed[span, :] = prim
            normed[rows + h * hrows : rows + (h + 1) * hrows, :] = tang

    inbuf[...] = latent[...].astype(F32)
    norm_all()
    for h in range(HALVES):
        state[h] = latent[own_rows(h), :].astype(F32)

    pl.semaphore_wait(barrier, n + m - 2)

    half = cols // 2
    core = lax.rem(s, 2)
    mine = pl.ds(pl.multiple_of(core * half, half), half)
    other = pl.ds(pl.multiple_of((1 - core) * half, half), half)
    partner = flip(1)
    loads[3].wait()
    w_copies = []
    for d in range(1, m):
        copy = remote(
            wout.at[z, mine], wout.at[z, mine], wsend.at[0, d], wrecv.at[0, d], s, zpeer(d)
        )
        copy.start()
        w_copies.append(copy)

    def kv_exchange(k):
        bufs = (kbuf, vbuf)
        sends = []

        def give(which, rel, slot, target, at):
            copy = remote(
                bufs[which].at[k, slot],
                bufs[which].at[k, slot],
                kvsend.at[k, which, len(sends)],
                kvrecv.at[k, which, at],
                target,
                z,
            )
            copy.start()
            sends.append(copy)

        def got(which, slot, at):
            pltpu.make_async_copy(
                bufs[which].at[k, slot], bufs[which].at[k, slot], kvrecv.at[k, which, at]
            ).wait()

        xn, yn = flip(2), flip(4)
        dn = yn + 2 - 4 * lax.rem(yn // 2, 2)

        def own(which):
            if n == 8:
                first, second = ((xn, 2), (yn, 4)) if which == 0 else ((yn, 4), (xn, 2))
                give(which, 0, s, *first)
                give(which, 0, s, *second)
                give(which, 0, s, partner, 1)
            else:
                for d in range(1, n):
                    give(which, d, s, lax.rem(s + d, n), d)

        def rest():
            if n != 8:
                return [[(w, lax.rem(s + n - d, n), d) for d in range(1, n)] for w in range(2)]
            got(0, xn, 2)
            give(0, 2, xn, yn, 6)
            give(0, 2, xn, partner, 3)
            got(1, yn, 4)
            give(1, 4, yn, xn, 6)
            give(1, 4, yn, partner, 5)
            got(0, yn, 4)
            give(0, 4, yn, partner, 5)
            got(1, xn, 2)
            give(1, 2, xn, partner, 3)
            got(0, dn, 6)
            give(0, 6, dn, partner, 7)
            got(1, dn, 6)
            give(1, 6, dn, partner, 7)

            def across(base):
                return base + 1 - 2 * lax.rem(base, 2)

            slots = ((s, 1), (xn, 3), (yn, 5), (dn, 7))
            return [[(w, across(t), r) for t, r in slots] for w in range(2)]

        return sends, own, rest, got

    lane = lax.broadcasted_iota(jnp.int32, (1, LANES), 1)
    scale = HEAD_DIM ** (-0.5)
    frames = rows * n
    trace = [None] * HALVES

    for k in range(STEPS):

        def project(which):
            if k == 0:
                loads[which].wait()
            weight = wqkv[:, which * cols : (which + 1) * cols]
            return dot(normed[...], weight).astype(BF16).reshape(2, rows, cols)

        def z_start(phase, src_of, dst):
            copies = []
            for d in range(m - 1, 0, -1):
                copy = remote(
                    src_of(zpeer(d)),
                    dst,
                    zsend.at[k, phase, d],
                    zrecv.at[k, phase, d],
                    s,
                    zpeer(d),
                )
                copy.start()
                copies.append(copy)
            return copies

        def z_wait(copies):
            for copy in copies:
                copy.wait_send()
                copy.wait_recv()

        sends, own, rest, got = kv_exchange(k)
        kbuf[k, s] = project(1)
        own(0)
        vbuf[k, s] = project(2)
        own(1)
        qbuf[...] = project(0)
        if k == 0:
            loads[5].wait()
            probe_down[...] = dot_t(probe[...], wdown[...])
        for group in rest():
            for item in group:
                got(*item)

        head_copies = []
        for h in range(HALVES):
            span = slice(h * hrows, (h + 1) * hrows)

            @pl.loop(0, pairs)
            def _(p):
                at = pl.ds(pl.multiple_of(p * LANES, LANES), LANES)
                keys = kbuf[k, :, 0, :, at].reshape(frames, LANES)
                key_tang = kbuf[k, :, 1, :, at].reshape(frames, LANES)
                vals = vbuf[k, :, 0, :, at].reshape(frames, LANES)
                val_tang = vbuf[k, :, 1, :, at].reshape(frames, LANES)
                both_keys = jnp.concatenate([keys, key_tang], axis=1)
                both_vals = jnp.concatenate([vals, val_tang], axis=1)
                queries = qbuf[0, span, at]
                query_tang = qbuf[1, span, at]
                zero = jnp.zeros_like(queries)
                left = []
                for side in range(LANES // HEAD_DIM):
                    keep = (lane // HEAD_DIM) == side
                    q = jnp.where(keep, queries, zero)
                    qt = jnp.where(keep, query_tang, zero)
                    left.append(
                        (
                            jnp.concatenate([q, zero], axis=1),
                            jnp.concatenate([qt, q], axis=1),
                        )
                    )
                stack = [item[0] for item in left] + [item[1] for item in left]
                both = dot_t(jnp.concatenate(stack, axis=0), both_keys) * scale
                scores, score_tang = both[: 2 * hrows], both[2 * hrows :]
                weights = jnp.exp(scores - jnp.max(scores, axis=-1, keepdims=True))
                weighted = weights * score_tang
                total = jnp.sum(weights, axis=-1, keepdims=True)
                carried = jnp.sum(weighted, axis=-1, keepdims=True)
                rounded = jnp.concatenate([weights.astype(BF16), weighted.astype(BF16)], axis=0)
                mixed = dot(rounded, both_vals)
                prim = mixed[: 2 * hrows, :LANES] / total
                tang = (mixed[2 * hrows :, :LANES] + mixed[: 2 * hrows, LANES:]) / total - (
                    carried / total
                ) * prim
                first = (lane // HEAD_DIM) == 0
                headall[k, h, z, 0, :, at] = jnp.where(first, prim[:hrows], prim[hrows:]).astype(
                    BF16
                )
                headall[k, h, z, 1, :, at] = jnp.where(first, tang[:hrows], tang[hrows:]).astype(
                    BF16
                )

            head_copies.append(z_start(h, lambda j: headall.at[k, h, z], headall.at[k, h, z]))

        if k == 0:
            forwards = []
            for d, copy in zip(range(1, m), w_copies):
                copy.wait_send()
                copy.wait_recv()
                forward = remote(
                    wout.at[zfrom(d), mine],
                    wout.at[zfrom(d), mine],
                    wsend.at[1, d],
                    wrecv.at[1, d],
                    partner,
                    z,
                )
                forward.start()
                forwards.append(forward)
            loads[4].wait()
            for forward in forwards:
                forward.wait_send()
                forward.wait_recv()

        rs_copies = []
        for h in range(HALVES):
            span = slice(h * hrows, (h + 1) * hrows)
            z_wait(head_copies[h])
            attn_both = jnp.zeros((2 * hrows, width), F32)
            for j in range(m):
                attn_both = attn_both + dot(
                    headall[k, h, j].reshape(2 * hrows, cols), wout[j]
                )
            attn, attn_tang = attn_both[:hrows], attn_both[hrows:]
            direction = probe[span, :].astype(F32)
            pair = norm_pair(inbuf[span, :] + attn, direction + attn_tang, gain_mlp[...])
            pre = dot(jnp.concatenate(pair, axis=0), win[...])
            act, act_tang = gelu_pair(pre[:hrows], pre[hrows:])
            terms = dot(act, wdown[...])
            rssend[k, h] = terms.astype(BF16).reshape(m, part, width)
            rs_copies.append(
                z_start(HALVES + h, lambda j: rssend.at[k, h, j], rsrecv.at[k, h, z])
            )
            partial[h] = (attn + terms).reshape(m, part, width)
            grown = jnp.sum(direction * attn_tang, axis=-1, keepdims=True) / m + jnp.sum(
                act_tang.astype(F32) * probe_down[span, :], axis=-1, keepdims=True
            )
            trace[h] = grown if k == 0 else trace[h] + grown

        last = k == STEPS - 1
        if last:
            column = jnp.concatenate(trace, axis=0) / (STEPS * width)
            trace_sum = jnp.sum(column, axis=0, keepdims=True)
            tracebuf[z] = jnp.transpose(jnp.broadcast_to(column, (rows, LANES)))[:8, :]
            trace_copies = []
            for d in range(1, m):
                copy = remote(
                    tracebuf.at[z], tracebuf.at[z], ssend.at[0, d], srecv.at[0, d], s, zpeer(d)
                )
                copy.start()
                trace_copies.append(copy)

        delta_copies = []
        squares = jnp.zeros((1, 1), F32)
        for h in range(HALVES):
            z_wait(rs_copies[h])
            field = partial[h, z]
            for d in range(1, m):
                field = field + rsrecv[k, h, zfrom(d)].astype(F32)
            new_state = state[h] + field / STEPS
            state[h] = new_state
            delta[k, h, z] = (new_state - latent[own_rows(h), :].astype(F32)).astype(BF16)
            delta_copies.append(
                z_start(2 * HALVES + h, lambda j: delta.at[k, h, z], delta.at[k, h, z])
            )
            if last:
                by_row = jnp.sum(new_state * new_state, axis=-1, keepdims=True)
                squares = squares + jnp.sum(by_row, axis=0, keepdims=True)
        for send in sends:
            send.wait_send()
        if last:
            share = trace_sum - 0.5 * squares / width
            tilebuf[z] = jnp.broadcast_to(share, (8, LANES))
            tile_copies = []
            for d in range(1, m):
                copy = remote(
                    tilebuf.at[z], tilebuf.at[z], ssend.at[1, d], srecv.at[1, d], s, zpeer(d)
                )
                copy.start()
                tile_copies.append(copy)
            z_wait(trace_copies)
            trace_row = jnp.sum(tracebuf[...], axis=0)
            z_wait(tile_copies)
            sumbuf[s] = jnp.sum(tilebuf[...], axis=0)
            mean_copies = []
            for d in range(1, n):
                copy = remote(
                    sumbuf.at[s], sumbuf.at[s], msend.at[d], mrecv.at[d], lax.rem(s + d, n), z
                )
                copy.start()
                mean_copies.append(copy)
        norms = []
        for h in range(HALVES):
            span = slice(h * hrows, (h + 1) * hrows)
            z_wait(delta_copies[h])
            following = latent[span, :].astype(F32) + delta[k, h].reshape(hrows, width).astype(F32)
            if last:
                latent_end[span, :] = following
                norms.append(jnp.sum(following * following, axis=-1, keepdims=True))
            else:
                following = following + ((k + 1) / STEPS) * time_embed[...]
                inbuf[span, :] = following
                prim, tang = norm_pair(following, probe[span, :].astype(F32), gain_attn[...])
                normed[span, :] = prim
                normed[rows + h * hrows : rows + (h + 1) * hrows, :] = tang
    norm_row = jnp.transpose(jnp.broadcast_to(jnp.concatenate(norms, axis=0), (rows, LANES)))[:8]
    half_log = 0.5 * math.log(2.0 * math.pi)
    first_row = lax.broadcasted_iota(jnp.int32, (8, rows), 0) == 0
    stats_out[...] = jnp.where(
        first_row, trace_row, trace_row - 0.5 * norm_row / width - half_log
    )
    z_wait(mean_copies)
    mean_out[...] = jnp.sum(sumbuf[...], axis=0) / frames - half_log


def per_device(
    n,
    m,
    latent,
    probe,
    time_embed,
    gain_attn,
    w_query,
    w_key,
    w_value,
    w_out,
    gain_mlp,
    w_in,
    w_down,
):
    rows, width = latent.shape
    cols = w_query.shape[1]
    hidden = w_in.shape[1]
    hrows = rows // HALVES
    part = hrows // m
    vmem = pl.BlockSpec(memory_space=pltpu.VMEM)
    anyspace = pl.BlockSpec(memory_space=pl.ANY)
    dma = pltpu.SemaphoreType.DMA
    state, stats, mean = pl.pallas_call(
        functools.partial(flow_kernel, n, m),
        out_shape=(
            jax.ShapeDtypeStruct((rows, width), F32),
            jax.ShapeDtypeStruct((8, rows), F32),
            jax.ShapeDtypeStruct((8, LANES), F32),
        ),
        in_specs=[vmem] * 5 + [anyspace] * 6,
        out_specs=(vmem, vmem, vmem),
        scratch_shapes=[
            pltpu.VMEM((width, 3 * cols), BF16),
            pltpu.VMEM((m, cols, width), BF16),
            pltpu.VMEM((width, hidden), BF16),
            pltpu.VMEM((hidden, width), BF16),
            pltpu.VMEM((2 * rows, width), BF16),
            pltpu.VMEM((2, rows, cols), BF16),
            pltpu.VMEM((STEPS, n, 2, rows, cols), BF16),
            pltpu.VMEM((STEPS, n, 2, rows, cols), BF16),
            pltpu.VMEM((STEPS, HALVES, m, 2, hrows, cols), BF16),
            pltpu.VMEM((rows, width), F32),
            pltpu.VMEM((rows, hidden), F32),
            pltpu.VMEM((HALVES, m, part, width), F32),
            pltpu.VMEM((STEPS, HALVES, m, part, width), BF16),
            pltpu.VMEM((STEPS, HALVES, m, part, width), BF16),
            pltpu.VMEM((HALVES, part, width), F32),
            pltpu.VMEM((STEPS, HALVES, m, part, width), BF16),
            pltpu.VMEM((m, 8, rows), F32),
            pltpu.VMEM((m, 8, LANES), F32),
            pltpu.VMEM((n, 8, LANES), F32),
            dma((6,)),
            dma((2, m)),
            dma((2, m)),
            dma((STEPS, 2, 2 * n)),
            dma((STEPS, 2, n)),
            dma((STEPS, 3 * HALVES, m)),
            dma((STEPS, 3 * HALVES, m)),
            dma((2, m)),
            dma((2, m)),
            dma((n,)),
            dma((n,)),
        ],
        compiler_params=pltpu.CompilerParams(
            collective_id=0, has_side_effects=True, vmem_limit_bytes=60 * 1024 * 1024
        ),
    )(
        latent,
        probe,
        time_embed.reshape(1, width),
        gain_attn.reshape(1, width),
        gain_mlp.reshape(1, width),
        w_query,
        w_key,
        w_value,
        w_out,
        w_in,
        w_down,
    )
    return (state, stats[0], stats[1], mean[0, 0])


def solution(mesh):
    return jax.shard_map(
        functools.partial(per_device, mesh.shape["seq"], mesh.shape["head"]),
        mesh=mesh,
        in_specs=(
            P("seq", None),
            P("seq", None),
            P(),
            P(),
            P(None, "head"),
            P(None, "head"),
            P(None, "head"),
            P("head", None),
            P(),
            P(None, "head"),
            P("head", None),
        ),
        out_specs=(P("seq", None), P("seq"), P("seq"), P()),
        check_vma=False,
    )
```

time: 140 us -> 105 us (0.75)
  Pallas kernels: 134 us -> 100 us
    pallas_call x1, Pallas kernels: 134 us -> 100 us  [per_device(): pl.pallas_call(functools.partial(flow_kernel, n, m), out_shape=(jax.Shape...]
where the time goes in v2:
time: 105 us
  Pallas kernels  100 us (95%)
  local copies, waits for them, and re-layouts  4.34 us (4%)
    pallas_call x1, Pallas kernels, per_device(): pl.pallas_call(functools.partial(flow_kernel, n, m), out_shape=(jax.Shape...  100 us

profile of v2, /device:TPU:0, one launch (start us, length us, event | category | flops | bytes accessed | tf_op | source)
XLA Modules:
  0.0 105.2 jit_solution(25668222601743219)
XLA Ops:
  0.6 100.2 %shard_map.138 = (f32[128,1024]{1,0:T(8,128)}, f32[8,128]{1,0:T(8,128)}, f32[8,128]{1,0:T(8,128)}) custom-call(bf16[128,1024]{1,0:T(8,128)(2,1)} %latent.1, bf16[128,1024]{1,0:T(8,128)(2,1)} %probe.1, f32[1,1024]{1,0:T(1,128)} %bitcast.8, f32[1,1024]{1,0:T(1,128)} %bitcast.9, f32[1,1024]{1,0:T(1,128)} %bitcast.10, bf16[1024,256]{1,0:T(8,128)(2,1)} %w_query.1, ...), custom_call_target="tpu_custom_call" | custom-call | tf_op jit(solution)/shard_map/pallas_call | solution.py:479
  100.8 1.2 %slice.11 = f32[1,1]{1,0:T(1,128)} slice(f32[8,128]{1,0:T(8,128)} %get-tuple-element.9), slice={[0:1], [0:1]} | slice | bytes 8 | tf_op jit(solution)/shard_map/slice | solution.py:536
  102.0 1.3 %slice_bitcast_fusion = (f32[128]{0:T(128)}, f32[128]{0:T(128)}) fusion(f32[8,128]{1,0:T(8,128)} %get-tuple-element.8), kind=kLoop, calls=%fused_computation | loop fusion | bytes 2048 | tf_op jit(solution)/shard_map/squeeze | solution.py:536
  103.3 1.9 %copy.16 = f32[128,1024]{1,0:T(8,128)} copy(f32[128,1024]{1,0:T(8,128)} %get-tuple-element.16) | data formatting | bytes 1048576

commit v3 on v2

--- a/solution.py
+++ b/solution.py
@@ -129,8 +129,8 @@
         pltpu.make_async_copy(w_in, win, wsem.at[4]),
         pltpu.make_async_copy(w_down, wdown, wsem.at[5]),
     ]
-    for load in loads:
-        load.start()
+    for index in (1, 2, 3, 0, 5, 4):
+        loads[index].start()
 
     barrier = pltpu.get_barrier_semaphore()
     for d in range(1, m):
@@ -165,27 +165,30 @@
     half = cols // 2
     core = lax.rem(s, 2)
     mine = pl.ds(pl.multiple_of(core * half, half), half)
-    other = pl.ds(pl.multiple_of((1 - core) * half, half), half)
+    quarter = half // 2
+    turn = lax.rem(s // 2, 2) * (1 - core) + lax.rem(s // 4, 2) * core
+    buddy = flip(2) * (1 - core) + flip(4) * core
+    fetched = pl.ds(pl.multiple_of(core * half + turn * quarter, quarter), quarter)
     partner = flip(1)
     loads[3].wait()
     w_copies = []
     for d in range(1, m):
         copy = remote(
-            wout.at[z, mine], wout.at[z, mine], wsend.at[0, d], wrecv.at[0, d], s, zpeer(d)
+            wout.at[z, fetched], wout.at[z, fetched], wsend.at[0, d], wrecv.at[0, d], s, zpeer(d)
         )
         copy.start()
         w_copies.append(copy)
 
-    def kv_exchange(k):
+    def kv_exchange(k, p):
         bufs = (kbuf, vbuf)
         sends = []
 
-        def give(which, rel, slot, target, at):
+        def give(which, slot, target, at):
             copy = remote(
-                bufs[which].at[k, slot],
-                bufs[which].at[k, slot],
-                kvsend.at[k, which, len(sends)],
-                kvrecv.at[k, which, at],
+                bufs[which].at[k, p, slot],
+                bufs[which].at[k, p, slot],
+                kvsend.at[k, p, len(sends)],
+                kvrecv.at[k, p, which, at],
                 target,
                 z,
             )
@@ -194,7 +197,7 @@
 
         def got(which, slot, at):
             pltpu.make_async_copy(
-                bufs[which].at[k, slot], bufs[which].at[k, slot], kvrecv.at[k, which, at]
+                bufs[which].at[k, p, slot], bufs[which].at[k, p, slot], kvrecv.at[k, p, which, at]
             ).wait()
 
         xn, yn = flip(2), flip(4)
@@ -203,38 +206,42 @@
         def own(which):
             if n == 8:
                 first, second = ((xn, 2), (yn, 4)) if which == 0 else ((yn, 4), (xn, 2))
-                give(which, 0, s, *first)
-                give(which, 0, s, *second)
-                give(which, 0, s, partner, 1)
+                give(which, s, *first)
+                give(which, s, *second)
+                give(which, s, partner, 1)
             else:
                 for d in range(1, n):
-                    give(which, d, s, lax.rem(s + d, n), d)
+                    give(which, s, lax.rem(s + d, n), d)
+
+        def relay():
+            if n == 8:
+                got(0, xn, 2)
+                give(0, xn, yn, 6)
+                got(1, yn, 4)
+                give(1, yn, xn, 6)
+                give(0, xn, partner, 3)
+                give(1, yn, partner, 5)
 
         def rest():
-            if n != 8:
-                return [[(w, lax.rem(s + n - d, n), d) for d in range(1, n)] for w in range(2)]
-            got(0, xn, 2)
-            give(0, 2, xn, yn, 6)
-            give(0, 2, xn, partner, 3)
-            got(1, yn, 4)
-            give(1, 4, yn, xn, 6)
-            give(1, 4, yn, partner, 5)
-            got(0, yn, 4)
-            give(0, 4, yn, partner, 5)
-            got(1, xn, 2)
-            give(1, 2, xn, partner, 3)
-            got(0, dn, 6)
-            give(0, 6, dn, partner, 7)
-            got(1, dn, 6)
-            give(1, 6, dn, partner, 7)
-
-            def across(base):
-                return base + 1 - 2 * lax.rem(base, 2)
-
-            slots = ((s, 1), (xn, 3), (yn, 5), (dn, 7))
-            return [[(w, across(t), r) for t, r in slots] for w in range(2)]
-
-        return sends, own, rest, got
+            if n == 8:
+                got(0, yn, 4)
+                give(0, yn, partner, 5)
+                got(1, xn, 2)
+                give(1, xn, partner, 3)
+                got(0, dn, 6)
+                give(0, dn, partner, 7)
+                got(1, dn, 6)
+                give(1, dn, partner, 7)
+                slots = ((s, 1), (xn, 3), (yn, 5), (dn, 7))
+                for which in range(2):
+                    for slot, at in slots:
+                        got(which, slot + 1 - 2 * lax.rem(slot, 2), at)
+            else:
+                for which in range(2):
+                    for d in range(1, n):
+                        got(which, lax.rem(s + n - d, n), d)
+
+        return sends, own, relay, rest
 
     lane = lax.broadcasted_iota(jnp.int32, (1, LANES), 1)
     scale = HEAD_DIM ** (-0.5)
@@ -269,30 +276,53 @@
                 copy.wait_send()
                 copy.wait_recv()
 
-        sends, own, rest, got = kv_exchange(k)
-        kbuf[k, s] = project(1)
-        own(0)
-        vbuf[k, s] = project(2)
-        own(1)
+        exchanges = [kv_exchange(k, p) for p in range(pairs)]
+
+        def keep_pairs(ref, both):
+            for p in range(pairs):
+                ref[k, p, s] = both[:, :, p * LANES : (p + 1) * LANES]
+
+        keep_pairs(kbuf, project(1))
+        exchanges[0][1](0)
+        keep_pairs(vbuf, project(2))
+        exchanges[0][1](1)
         qbuf[...] = project(0)
+        exchanges[0][2]()
+        for p in range(1, pairs):
+            exchanges[p][1](0)
+            exchanges[p][1](1)
         if k == 0:
             loads[5].wait()
             probe_down[...] = dot_t(probe[...], wdown[...])
-        for group in rest():
-            for item in group:
-                got(*item)
-
-        head_copies = []
-        for h in range(HALVES):
-            span = slice(h * hrows, (h + 1) * hrows)
-
-            @pl.loop(0, pairs)
-            def _(p):
-                at = pl.ds(pl.multiple_of(p * LANES, LANES), LANES)
-                keys = kbuf[k, :, 0, :, at].reshape(frames, LANES)
-                key_tang = kbuf[k, :, 1, :, at].reshape(frames, LANES)
-                vals = vbuf[k, :, 0, :, at].reshape(frames, LANES)
-                val_tang = vbuf[k, :, 1, :, at].reshape(frames, LANES)
+
+        def w_pass(stage, which, target):
+            copies = []
+            for d in range(1, m):
+                copy = remote(
+                    wout.at[zfrom(d), which],
+                    wout.at[zfrom(d), which],
+                    wsend.at[stage, d],
+                    wrecv.at[stage, d],
+                    target,
+                    z,
+                )
+                copy.start()
+                copies.append(copy)
+            return copies
+
+        head_copies = [[] for _ in range(HALVES)]
+        for p in range(pairs):
+            if k == 0 and p == pairs - 1:
+                z_wait(w_copies)
+                w_trades = w_pass(1, fetched, buddy)
+            exchanges[p][3]()
+            for h in range(HALVES):
+                span = slice(h * hrows, (h + 1) * hrows)
+                at = slice(p * LANES, (p + 1) * LANES)
+                keys = kbuf[k, p, :, 0].reshape(frames, LANES)
+                key_tang = kbuf[k, p, :, 1].reshape(frames, LANES)
+                vals = vbuf[k, p, :, 0].reshape(frames, LANES)
+                val_tang = vbuf[k, p, :, 1].reshape(frames, LANES)
                 both_keys = jnp.concatenate([keys, key_tang], axis=1)
                 both_vals = jnp.concatenate([vals, val_tang], axis=1)
                 queries = qbuf[0, span, at]
@@ -323,44 +353,33 @@
                     carried / total
                 ) * prim
                 first = (lane // HEAD_DIM) == 0
-                headall[k, h, z, 0, :, at] = jnp.where(first, prim[:hrows], prim[hrows:]).astype(
+                headall[k, h, p, z, 0] = jnp.where(first, prim[:hrows], prim[hrows:]).astype(
                     BF16
                 )
-                headall[k, h, z, 1, :, at] = jnp.where(first, tang[:hrows], tang[hrows:]).astype(
+                headall[k, h, p, z, 1] = jnp.where(first, tang[:hrows], tang[hrows:]).astype(
                     BF16
                 )
 
-            head_copies.append(z_start(h, lambda j: headall.at[k, h, z], headall.at[k, h, z]))
+                head_copies[h] += z_start(
+                    p * HALVES + h, lambda j: headall.at[k, h, p, z], headall.at[k, h, p, z]
+                )
+                if h == 0 and p + 1 < pairs:
+                    exchanges[p + 1][2]()
 
         if k == 0:
-            forwards = []
-            for d, copy in zip(range(1, m), w_copies):
-                copy.wait_send()
-                copy.wait_recv()
-                forward = remote(
-                    wout.at[zfrom(d), mine],
-                    wout.at[zfrom(d), mine],
-                    wsend.at[1, d],
-                    wrecv.at[1, d],
-                    partner,
-                    z,
-                )
-                forward.start()
-                forwards.append(forward)
+            z_wait(w_trades)
+            forwards = w_pass(2, mine, partner)
             loads[4].wait()
-            for forward in forwards:
-                forward.wait_send()
-                forward.wait_recv()
+            z_wait(forwards)
 
         rs_copies = []
         for h in range(HALVES):
             span = slice(h * hrows, (h + 1) * hrows)
             z_wait(head_copies[h])
-            attn_both = jnp.zeros((2 * hrows, width), F32)
-            for j in range(m):
-                attn_both = attn_both + dot(
-                    headall[k, h, j].reshape(2 * hrows, cols), wout[j]
-                )
+            heads = [
+                headall[k, h, p, j].reshape(2 * hrows, LANES) for j in range(m) for p in range(pairs)
+            ]
+            attn_both = dot(jnp.concatenate(heads, axis=1), wout[...].reshape(m * cols, width))
             attn, attn_tang = attn_both[:hrows], attn_both[hrows:]
             direction = probe[span, :].astype(F32)
             pair = norm_pair(inbuf[span, :] + attn, direction + attn_tang, gain_mlp[...])
@@ -369,7 +388,7 @@
             terms = dot(act, wdown[...])
             rssend[k, h] = terms.astype(BF16).reshape(m, part, width)
             rs_copies.append(
-                z_start(HALVES + h, lambda j: rssend.at[k, h, j], rsrecv.at[k, h, z])
+                z_start(pairs * HALVES + h, lambda j: rssend.at[k, h, j], rsrecv.at[k, h, z])
             )
             partial[h] = (attn + terms).reshape(m, part, width)
             grown = jnp.sum(direction * attn_tang, axis=-1, keepdims=True) / m + jnp.sum(
@@ -401,13 +420,14 @@
             state[h] = new_state
             delta[k, h, z] = (new_state - latent[own_rows(h), :].astype(F32)).astype(BF16)
             delta_copies.append(
-                z_start(2 * HALVES + h, lambda j: delta.at[k, h, z], delta.at[k, h, z])
+                z_start((pairs + 1) * HALVES + h, lambda j: delta.at[k, h, z], delta.at[k, h, z])
             )
             if last:
                 by_row = jnp.sum(new_state * new_state, axis=-1, keepdims=True)
                 squares = squares + jnp.sum(by_row, axis=0, keepdims=True)
-        for send in sends:
-            send.wait_send()
+        for exchange in exchanges:
+            for send in exchange[0]:
+                send.wait_send()
         if last:
             share = trace_sum - 0.5 * squares / width
             tilebuf[z] = jnp.broadcast_to(share, (8, LANES))
@@ -473,6 +493,7 @@
     hidden = w_in.shape[1]
     hrows = rows // HALVES
     part = hrows // m
+    pairs = cols // LANES
     vmem = pl.BlockSpec(memory_space=pltpu.VMEM)
     anyspace = pl.BlockSpec(memory_space=pl.ANY)
     dma = pltpu.SemaphoreType.DMA
@@ -492,9 +513,9 @@
             pltpu.VMEM((hidden, width), BF16),
             pltpu.VMEM((2 * rows, width), BF16),
             pltpu.VMEM((2, rows, cols), BF16),
-            pltpu.VMEM((STEPS, n, 2, rows, cols), BF16),
-            pltpu.VMEM((STEPS, n, 2, rows, cols), BF16),
-            pltpu.VMEM((STEPS, HALVES, m, 2, hrows, cols), BF16),
+            pltpu.VMEM((STEPS, pairs, n, 2, rows, LANES), BF16),
+            pltpu.VMEM((STEPS, pairs, n, 2, rows, LANES), BF16),
+            pltpu.VMEM((STEPS, HALVES, pairs, m, 2, hrows, LANES), BF16),
             pltpu.VMEM((rows, width), F32),
             pltpu.VMEM((rows, hidden), F32),
             pltpu.VMEM((HALVES, m, part, width), F32),
@@ -506,12 +527,12 @@
             pltpu.VMEM((m, 8, LANES), F32),
             pltpu.VMEM((n, 8, LANES), F32),
             dma((6,)),
-            dma((2, m)),
-            dma((2, m)),
-            dma((STEPS, 2, 2 * n)),
-            dma((STEPS, 2, n)),
-            dma((STEPS, 3 * HALVES, m)),
-            dma((STEPS, 3 * HALVES, m)),
+            dma((3, m)),
+            dma((3, m)),
+            dma((STEPS, pairs, 2 * n)),
+            dma((STEPS, pairs, 2, n)),
+            dma((STEPS, (pairs + 2) * HALVES, m)),
+            dma((STEPS, (pairs + 2) * HALVES, m)),
             dma((2, m)),
             dma((2, m)),
             dma((n,)),

time: 105 us -> 94.1 us (0.90)
  Pallas kernels: 100 us -> 88.8 us
    pallas_call x1, Pallas kernels: 100 us -> 88.8 us  [per_device(): pl.pallas_call(functools.partial(flow_kernel, n, m), out_shape=(jax.Shape...]
where the time goes in v3:
time: 94.1 us; the launch traced here: 93.8 us
  Pallas kernels  88.8 us (94%)
  local copies, waits for them, and re-layouts  4.34 us (5%)
    pallas_call x1, Pallas kernels, per_device(): pl.pallas_call(functools.partial(flow_kernel, n, m), out_shape=(jax.Shape...  88.8 us
    unnamed x1, local copies, waits for them, and re-layouts  1.88 us

profile of v3, /device:TPU:0, one launch (start us, length us, event | category | flops | bytes accessed | tf_op | source)
XLA Modules:
  0.0 93.8 jit_solution(1907253678768312564)
XLA Ops:
  0.6 88.8 %shard_map.138 = (f32[128,1024]{1,0:T(8,128)}, f32[8,128]{1,0:T(8,128)}, f32[8,128]{1,0:T(8,128)}) custom-call(bf16[128,1024]{1,0:T(8,128)(2,1)} %latent.1, bf16[128,1024]{1,0:T(8,128)(2,1)} %probe.1, f32[1,1024]{1,0:T(1,128)} %bitcast.8, f32[1,1024]{1,0:T(1,128)} %bitcast.9, f32[1,1024]{1,0:T(1,128)} %bitcast.10, bf16[1024,256]{1,0:T(8,128)(2,1)} %w_query.1, ...), custom_call_target="tpu_custom_call" | custom-call | tf_op jit(solution)/shard_map/pallas_call | solution.py:500
  89.5 1.2 %slice.11 = f32[1,1]{1,0:T(1,128)} slice(f32[8,128]{1,0:T(8,128)} %get-tuple-element.9), slice={[0:1], [0:1]} | slice | bytes 8 | tf_op jit(solution)/shard_map/slice | solution.py:557
  90.6 1.3 %slice_bitcast_fusion = (f32[128]{0:T(128)}, f32[128]{0:T(128)}) fusion(f32[8,128]{1,0:T(8,128)} %get-tuple-element.8), kind=kLoop, calls=%fused_computation | loop fusion | bytes 2048 | tf_op jit(solution)/shard_map/squeeze | solution.py:557
  91.9 1.9 %copy.16 = f32[128,1024]{1,0:T(8,128)} copy(f32[128,1024]{1,0:T(8,128)} %get-tuple-element.16) | data formatting | bytes 1048576
